TPU v7x, 256 devices: a whole 4x4x8 slice. The times are simulated.
256 devices in a mesh: gx: 8 (over z), gy: 4 (over x), gz: 8 (over y, core).
Axes of the slice: x: 4, y: 4, z: 8, core: 2. Of those that a mesh axis runs over, the one named last changes fastest.
Arguments:
- source: float32 [64, 128, 1024], P('gx', 'gy', 'gz'), may hold values from 0.05 to 1
- target: float32 [64, 128, 1024], P('gx', 'gy', 'gz'), may hold values from 0.05 to 1
- kernel_half: float32 [5], replicated, may hold values from 0.05 to 1
- smooth_half: float32 [9], replicated, may hold values from 0.1 to 1
Outputs:
- displacement: float32 [3, 64, 128, 1024], P(None, 'gx', 'gy', 'gz')
- mismatch: float32 [6], replicated
All inputs are finite; a program needn't handle non-finite values.
Results may differ from a plain program's by a relative error of at most 0.0001.
Values sent between devices are 32-bit elements; how exact they have to be, the bound alone decides.
A program may use at most 64 MiB of HBM per device.

v0:
```python
import functools

import jax
import jax.numpy as jnp
from jax import lax
from jax.experimental import pallas as pl
from jax.experimental.pallas import tpu as pltpu
from jax.sharding import PartitionSpec as P

ITERS = 6
R = 4
S = 8
BX, BY, BZ = 8, 32, 128
TY = BY // 8
MESH = pl.DeviceIdType.MESH
F32 = jnp.float32

DIRS = sorted(
    [
        (dx, dy, dz)
        for dx in (-1, 0, 1)
        for dy in (-1, 0, 1)
        for dz in (-1, 0, 1)
        if (dx, dy, dz) != (0, 0, 0)
    ],
    key=lambda d: (-sum(abs(c) for c in d), abs(d[0]), abs(d[1]), d),
)
YZ = [d for d in DIRS if d[0] == 0]


def kernel(
    sizes,
    src_hbm, tgt_hbm, kern, smo,
    disp_hbm, mis,
    a_ref, b_ref, f, zp, zb, t, tz, w, tots, totb, out,
    xb, yb, pz, zs, t2, tz2,
    send, recv, xsend, xrecv, ysend, yrecv, lsend, lrecv, loc,
):
    nx, ny, nz = sizes
    cells = float(nx * ny * nz * BX * BY * BZ)
    mx, my, mz = lax.axis_index("gx"), lax.axis_index("gy"), lax.axis_index("gz")
    pos = {"gx": (mx, nx), "gy": (my, ny), "gz": (mz, nz)}
    lane = lax.broadcasted_iota(jnp.int32, (8, BZ), 1)
    sub = lax.broadcasted_iota(jnp.int32, (8, BZ), 0)
    zero = jnp.zeros((8, BZ), F32)

    loads = [
        pltpu.make_async_copy(src_hbm, a_ref, loc.at[0]),
        pltpu.make_async_copy(tgt_hbm, b_ref, loc.at[1]),
    ]
    for c in loads:
        c.start()

    def inside(m, n, d):
        if d == 0:
            return None
        return m + d < n if d > 0 else m + d >= 0

    conds = [{d: inside(m, n, d) for d in (-1, 0, 1)} for m, n in pos.values()]

    def has(d):
        c = [conds[i][d[i]] for i in range(3) if d[i]]
        return functools.reduce(jnp.logical_and, c)

    def peer(d):
        ids = {}
        for axis, step in zip(pos, d):
            if step:
                ids[axis] = pos[axis][0] + step
        return ids

    def neg(d):
        return tuple(-c for c in d)

    for p in range(2):
        for i in range(2 * R + BX):
            for j in range(TY + 2):
                f[p, i, pl.ds(8 * j, 8), :] = zero
        for q in range(2):
            for e in range(3):
                for j in range(4):
                    zb[p, q, e, pl.ds(8 * j, 8), :] = zero

    barrier = pltpu.get_barrier_semaphore()
    expected = sum(n - 1 for _, n in pos.values())
    for axis, (m, n) in pos.items():
        for j in range(1, n):
            pl.semaphore_signal(
                barrier, 1, device_id={axis: lax.rem(m + j, n)}, device_id_type=MESH
            )
    for d in DIRS:
        if sum(abs(c) for c in d) > 1:
            there = has(d)
            expected = expected + jnp.where(there, 1, 0)

            @pl.when(there)
            def _():
                pl.semaphore_signal(barrier, 1, device_id=peer(d), device_id_type=MESH)

    k = [kern[i] for i in range(R + 1)]
    norm = smo[0]
    tail = smo[1]
    for i in range(2, S + 1):
        tail = tail + smo[i]
    norm = jnp.full((8, BZ), norm + 2.0 * tail, F32)
    s = [jnp.full((8, BZ), smo[i], F32) / norm for i in range(S + 1)]

    for c in range(3):
        for i in range(BX):
            for j in range(TY):
                xb[c, i, pl.ds(8 * j, 8), :] = zero
                xb[c, 2 * BX + i, pl.ds(8 * j, 8), :] = zero
            for j in (0, TY + 1):
                yb[c, i, pl.ds(8 * j, 8), :] = zero
        for q in range(2):
            for j in range(TY + 2):
                zs[c, q, pl.ds(8 * j, 8), :] = zero

    def copy(p, d):
        i = DIRS.index(d)
        dx, dy, dz = d
        if dz == 0:
            xs = {1: pl.ds(BX, R), -1: pl.ds(R, R), 0: pl.ds(R, BX)}[dx]
            xd = {1: pl.ds(0, R), -1: pl.ds(R + BX, R), 0: pl.ds(R, BX)}[dx]
            ys = {1: pl.ds(BY, 8), -1: pl.ds(8, 8), 0: pl.ds(8, BY)}[dy]
            yd = {1: pl.ds(0, 8), -1: pl.ds(BY + 8, 8), 0: pl.ds(8, BY)}[dy]
            source, target = f.at[p, xs, ys], f.at[p, xd, yd]
        else:
            side = 0 if dz > 0 else 1
            rows = {1: pl.ds(8, 8), -1: pl.ds(0, 8), 0: pl.ds(0, 16)}[dy]
            lands = {1: pl.ds(0, 8), -1: pl.ds(24, 8), 0: pl.ds(8, 16)}[dy]
            source, target = zp.at[p, rows], zb.at[p, side, 1 - dx, lands]
        return pltpu.make_async_remote_copy(
            src_ref=source, dst_ref=target, send_sem=send.at[p, i],
            recv_sem=recv.at[p, i], device_id=peer(d), device_id_type=MESH,
        )

    def start(p):
        for d in DIRS:
            @pl.when(has(d))
            def _():
                copy(p, d).start()

    def sent(p):
        for d in DIRS:
            @pl.when(has(d))
            def _():
                copy(p, d).wait_send()

    def arrived(p, dirs):
        for d in dirs:
            @pl.when(has(neg(d)))
            def _():
                copy(p, d).wait_recv()

    def line(axis, q, go):
        m, n = pos[axis]
        base = {"gx": 0, "gy": nx - 1, "gz": nx + ny - 2}[axis]
        for j in range(1, n):
            c = pltpu.make_async_remote_copy(
                src_ref=tots.at[q, "xyz".index(axis[1])], dst_ref=totb.at[q, base + j - 1],
                send_sem=lsend.at[q, base + j - 1], recv_sem=lrecv.at[q, base + j - 1],
                device_id={axis: lax.rem(m + j, n)}, device_id_type=MESH,
            )
            if go:
                c.start()
            else:
                c.wait()

    def line_end(axis, q):
        line(axis, q, False)
        n = pos[axis][1]
        a = "xyz".index(axis[1])
        base = {"gx": 0, "gy": nx - 1, "gz": nx + ny - 2}[axis]
        v = tots[q, a]
        for j in range(1, n):
            v = v + totb[q, base + j - 1]
        tots[q, a + 1] = v

    def symmetric(taps, at):
        acc = taps[0] * at(0)
        for d in range(1, len(taps)):
            acc = acc + taps[d] * (at(d) + at(-d))
        return acc

    def slope(taps, at):
        acc = None
        for d in range(1, len(taps)):
            term = (float(d) * taps[d]) * (at(d) - at(-d))
            acc = term if acc is None else acc + term
        return acc

    def roll(v, by):
        by = by % BZ
        return v if by == 0 else pltpu.roll(v, by, 1)

    def along_z(own, halo, taps, passes):
        n = len(taps)
        shifted = {0: own}
        for d in range(1, n):
            shifted[d] = roll(jnp.where(lane < d, halo, own), -d)
            shifted[-d] = roll(jnp.where(lane >= BZ - d, halo, own), d)
        return [q(taps, lambda d: shifted[d]) for q in passes]

    def packed_in(p):
        left = (lane % 8) < R
        tiles = []
        for e in range(4):
            rows = pl.ds(8 * e, 8)
            face = jnp.where(left, zb[p, 0, 1, rows, :], zb[p, 1, 1, rows, :])
            low = jnp.where(left, zb[p, 0, 0, rows, :], zb[p, 1, 0, rows, :])
            high = jnp.where(left, zb[p, 0, 2, rows, :], zb[p, 1, 2, rows, :])
            edge = jnp.where((lane % 64) >= 32, low, high)
            for h in {0: (1,), 1: (0, 1), 2: (0, 1), 3: (0,)}[e]:
                tiles.append(
                    jnp.where(
                        (lane >= 32) & (lane < 96),
                        roll(face, 32 - 64 * h),
                        roll(edge, 96 - 64 * h),
                    )
                )
        return tiles

    def x_pass(p, dst, passes):
        for j in range(TY + 2):
            rows = pl.ds(8 * j, 8)
            col = [f[p, i, rows, :] for i in range(2 * R + BX)]
            for i in range(BX):
                for n, q in enumerate(passes):
                    dst[n, i, rows, :] = q(k, lambda d: col[i + R + d])

    def x_pass_packed(p, dst, passes):
        for j, z in enumerate(packed_in(p)):
            moved = {d: roll(z, -8 * d) for d in range(-R, R + 1)}
            for n, q in enumerate(passes):
                dst[n, pl.ds(8 * j, 8), :] = q(k, lambda d: moved[d])

    def y_at(ref, j):
        return lambda d: ref[pl.ds(8 + 8 * j + d, 8), :]

    def pack_init():
        return {}

    def pack(acc, v, i, j):
        e, h = divmod(j, 2)
        at = 64 * h + 8 * i
        moved = roll(v, at + 4)
        acc[e] = moved if e not in acc else jnp.where((lane >= at) & (lane < at + 8), moved, acc[e])

    def apply(p, use):
        x_pass(p, t, [symmetric])
        x_pass_packed(p, tz, [symmetric])
        for j in range(TY):
            halos = symmetric(k, y_at(tz.at[0], j))
            for i in range(BX):
                own = symmetric(k, y_at(t.at[0, i], j))
                halo = roll(halos, -(8 * (i + R) + 4))
                use(i, j, along_z(own, halo, k, [symmetric])[0])

    def put(p, i, j, v, acc):
        f[p, R + i, pl.ds(8 + 8 * j, 8), :] = v
        pack(acc, v, i, j)

    def flush(p, acc):
        for e, v in acc.items():
            zp[p, pl.ds(8 * e, 8), :] = v

    def ones_sum(index, n):
        acc = None
        for d in range(-R, R + 1):
            ok = (index + d >= 0) & (index + d < n)
            term = jnp.where(ok, k[abs(d)], 0.0)
            acc = term if acc is None else acc + term
        return acc

    sum_z = ones_sum(lane + mz * BZ, nz * BZ)
    sum_y = [ones_sum(sub + (my * BY + 8 * j), ny * BY) * sum_z for j in range(TY)]
    sum_x = [ones_sum(mx * BX + i, nx * BX) for i in range(BX)]

    for c in loads:
        c.wait()
    acc = pack_init()
    total_a, total_b = zero, zero
    for j in range(TY):
        rows = pl.ds(8 * j, 8)
        for i in range(BX):
            a = a_ref[i, rows, :]
            total_a = total_a + a
            total_b = total_b + b_ref[i, rows, :]
            f[1, R + i, pl.ds(8 + 8 * j, 8), :] = jnp.ones((8, BZ), F32)
            put(0, i, j, a / (sum_x[i] * sum_y[j]), acc)
    flush(0, acc)
    tots[0, 0, pl.ds(0, 8), :] = total_a
    tots[0, 0, pl.ds(8, 8), :] = total_b
    pl.semaphore_wait(barrier, expected)
    start(0)
    line("gx", 0, True)

    def v_step(n):
        arrived(0, DIRS)
        acc = pack_init()

        def use(i, j, ku):
            v = f[1, R + i, pl.ds(8 + 8 * j, 8), :]
            w[n, i, pl.ds(8 * j, 8), :] = v * ku
            put(1, i, j, b_ref[i, pl.ds(8 * j, 8), :] / ku, acc)

        apply(0, use)
        flush(1, acc)
        start(1)
        sent(0)

    def u_step():
        arrived(1, DIRS)
        acc = pack_init()

        def use(i, j, kv):
            put(0, i, j, a_ref[i, pl.ds(8 * j, 8), :] / kv, acc)

        apply(1, use)
        flush(0, acc)
        start(0)
        sent(1)

    def iteration(n, carry):
        v_step(n)

        @pl.when(n == 1)
        def _():
            line_end("gx", 0)
            line("gy", 0, True)

        @pl.when(n == 3)
        def _():
            line_end("gy", 0)
            line("gz", 0, True)

        u_step()
        return carry

    lax.fori_loop(0, ITERS - 1, iteration, 0)
    v_step(ITERS - 1)

    line_end("gz", 0)

    def everything(v):
        return jnp.full((8, BZ), cells, F32) / jnp.full((8, BZ), jnp.sum(v), F32)

    alpha = everything(tots[0, 3, pl.ds(0, 8), :])
    beta = everything(tots[0, 3, pl.ds(8, 8), :])
    rows = zero
    for n in range(ITERS):
        part = zero
        for i in range(BX):
            for j in range(TY):
                at = pl.ds(8 * j, 8)
                part = part + jnp.abs(alpha * w[n, i, at, :] - beta * b_ref[i, at, :])
        part = jnp.broadcast_to(jnp.sum(part, axis=0, keepdims=True), (8, BZ))
        rows = jnp.where(sub == n, part, rows)
    tots[1, 0, pl.ds(0, 8), :] = rows
    tots[1, 0, pl.ds(8, 8), :] = zero
    line("gx", 1, True)

    arrived(1, DIRS)
    x_pass(1, t, [symmetric, slope])
    x_pass_packed(1, tz, [symmetric, slope])
    for j in range(TY):
        at = pl.ds(8 + 8 * j, 8)
        halos = [
            symmetric(k, y_at(tz.at[0], j)),
            slope(k, y_at(tz.at[0], j)),
            symmetric(k, y_at(tz.at[1], j)),
        ]
        for i in range(BX):
            by = -(8 * (i + R) + 4)
            kk, kg = symmetric(k, y_at(t.at[0, i], j)), slope(k, y_at(t.at[0, i], j))
            gk = symmetric(k, y_at(t.at[1, i], j))
            kvol, znum = along_z(kk, roll(halos[0], by), k, [symmetric, slope])
            ynum = along_z(kg, roll(halos[1], by), k, [symmetric])[0]
            xnum = along_z(gk, roll(halos[2], by), k, [symmetric])[0]
            inverse = 1.0 / kvol
            for c, num in enumerate((xnum, ynum, znum)):
                xb[c, BX + i, pl.ds(8 * j, 8), :] = num * inverse

    def x_copy(c, d):
        lands = 0 if d > 0 else 2 * BX
        e = 0 if d > 0 else 1
        return pltpu.make_async_remote_copy(
            src_ref=xb.at[c, pl.ds(BX, BX)], dst_ref=xb.at[c, pl.ds(lands, BX)],
            send_sem=xsend.at[c, e], recv_sem=xrecv.at[c, e],
            device_id={"gx": mx + d}, device_id_type=MESH,
        )

    def y_copy(c, d):
        i = YZ.index(d)
        _, dy, dz = d
        if dz == 0:
            ys = pl.ds(BY, 8) if dy > 0 else pl.ds(8, 8)
            yd = pl.ds(0, 8) if dy > 0 else pl.ds(BY + 8, 8)
            source, target = yb.at[c, :, ys], yb.at[c, :, yd]
        else:
            side = 0 if dz > 0 else 1
            rows = {1: pl.ds(BY - 8, 8), -1: pl.ds(0, 8), 0: pl.ds(0, BY)}[dy]
            lands = {1: pl.ds(0, 8), -1: pl.ds(BY + 8, 8), 0: pl.ds(8, BY)}[dy]
            source, target = pz.at[c, rows], zs.at[c, side, lands]
        return pltpu.make_async_remote_copy(
            src_ref=source, dst_ref=target, send_sem=ysend.at[c, i],
            recv_sem=yrecv.at[c, i], device_id=peer(d), device_id_type=MESH,
        )

    for c in range(3):
        for d in (-1, 1):
            @pl.when(conds[0][d])
            def _():
                x_copy(c, d).start()
    sent(1)
    line_end("gx", 1)
    line("gy", 1, True)

    stores = [pltpu.make_async_copy(out.at[c], disp_hbm.at[c], loc.at[2 + c]) for c in range(3)]

    for c in range(3):
        for d in (-1, 1):
            @pl.when(conds[0][-d])
            def _():
                x_copy(c, d).wait_recv()
        for j in range(TY):
            at = pl.ds(8 * j, 8)
            packed = None
            for i in range(BX):
                v = symmetric(s, lambda d: xb[c, BX + i + d, at, :])
                yb[c, i, pl.ds(8 + 8 * j, 8), :] = v
                moved = roll(v, 16 * i + 8)
                packed = moved if packed is None else jnp.where(
                    (lane >= 16 * i) & (lane < 16 * i + 16), moved, packed
                )
            pz[c, at, :] = packed
        for d in YZ:
            @pl.when(has(d))
            def _():
                y_copy(c, d).start()
        if c == 0:
            line_end("gy", 1)
            line("gz", 1, True)

    for c in range(3):
        for d in YZ:
            @pl.when(has(neg(d)))
            def _():
                y_copy(c, d).wait_recv()
        for j in range(TY + 2):
            at = pl.ds(8 * j, 8)
            tz2[at, :] = jnp.where((lane % 16) < S, zs[c, 0, at, :], zs[c, 1, at, :])
        for j in range(TY):
            halos = symmetric(s, y_at(tz2, j))
            for i in range(BX):
                own = symmetric(s, y_at(yb.at[c, i], j))
                out[c, i, pl.ds(8 * j, 8), :] = along_z(
                    own, roll(halos, -(16 * i + 8)), s, [symmetric]
                )[0]
        stores[c].start()

    line_end("gz", 1)
    done = tots[1, 3, pl.ds(0, 8), :]
    for n in range(ITERS):
        mis[n] = jnp.sum(jnp.where(sub == n, done, 0.0)) / cells
    for c in range(3):
        for d in (-1, 1):
            @pl.when(conds[0][d])
            def _():
                x_copy(c, d).wait_send()
        for d in YZ:
            @pl.when(has(d))
            def _():
                y_copy(c, d).wait_send()
        stores[c].wait()


def solution(mesh):
    sizes = tuple(mesh.shape[a] for a in ("gx", "gy", "gz"))
    peers = sum(sizes) - 3

    def step(source, target, kernel_half, smooth_half):
        return pl.pallas_call(
            functools.partial(kernel, sizes),
            out_shape=(
                jax.ShapeDtypeStruct((3, BX, BY, BZ), F32),
                jax.ShapeDtypeStruct((ITERS,), F32),
            ),
            in_specs=[
                pl.BlockSpec(memory_space=pl.ANY),
                pl.BlockSpec(memory_space=pl.ANY),
                pl.BlockSpec(memory_space=pltpu.SMEM),
                pl.BlockSpec(memory_space=pltpu.SMEM),
            ],
            out_specs=(
                pl.BlockSpec(memory_space=pl.ANY),
                pl.BlockSpec(memory_space=pltpu.SMEM),
            ),
            scratch_shapes=[
                pltpu.VMEM((BX, BY, BZ), F32),
                pltpu.VMEM((BX, BY, BZ), F32),
                pltpu.VMEM((2, BX + 2 * R, BY + 16, BZ), F32),
                pltpu.VMEM((2, 16, BZ), F32),
                pltpu.VMEM((2, 2, 3, 32, BZ), F32),
                pltpu.VMEM((2, BX, BY + 16, BZ), F32),
                pltpu.VMEM((2, BY + 16, BZ), F32),
                pltpu.VMEM((ITERS, BX, BY, BZ), F32),
                pltpu.VMEM((2, 4, 16, BZ), F32),
                pltpu.VMEM((2, peers, 16, BZ), F32),
                pltpu.VMEM((3, BX, BY, BZ), F32),
                pltpu.VMEM((3, 3 * BX, BY, BZ), F32),
                pltpu.VMEM((3, BX, BY + 16, BZ), F32),
                pltpu.VMEM((3, BY, BZ), F32),
                pltpu.VMEM((3, 2, BY + 16, BZ), F32),
                pltpu.VMEM((8, BZ), F32),
                pltpu.VMEM((BY + 16, BZ), F32),
                pltpu.SemaphoreType.DMA((2, 26)),
                pltpu.SemaphoreType.DMA((2, 26)),
                pltpu.SemaphoreType.DMA((3, 2)),
                pltpu.SemaphoreType.DMA((3, 2)),
                pltpu.SemaphoreType.DMA((3, 8)),
                pltpu.SemaphoreType.DMA((3, 8)),
                pltpu.SemaphoreType.DMA((2, peers)),
                pltpu.SemaphoreType.DMA((2, peers)),
                pltpu.SemaphoreType.DMA((5,)),
            ],
            compiler_params=pltpu.CompilerParams(
                collective_id=0, has_side_effects=True, vmem_limit_bytes=32 * 1024 * 1024
            ),
        )(source, target, kernel_half, smooth_half)

    placed = P("gx", "gy", "gz")
    return jax.shard_map(
        step,
        mesh=mesh,
        in_specs=(placed, placed, P(), P()),
        out_specs=(P(None, "gx", "gy", "gz"), P()),
        check_vma=False,
    )
```

profile of v0, /device:TPU:1, one launch (start us, length us, event | category | flops | bytes accessed | tf_op | source)
XLA Modules:
  0.0 105.4 jit_solution(3922631300370617393)
XLA Ops:
  0.6 0.0 copy-start
  0.6 0.9 copy-done
  1.5 0.0 copy-start.1
  1.5 0.9 copy-done.1
  2.4 0.0 copy-start.2
  2.4 0.7 copy-done.2
  3.1 0.0 copy-start.3
  3.1 0.7 copy-done.3
  3.8 100.4 %shard_map.59 = (f32[3,8,32,128]{3,2,1,0:T(8,128)S(1)}, f32[6]{0:T(128)S(1)}) custom-call(f32[8,32,128]{2,1,0:T(8,128)S(1)} %copy-done, f32[8,32,128]{2,1,0:T(8,128)S(1)} %copy-done.1, f32[5]{0:T(128)S(1)} %copy-done.2, f32[9]{0:T(128)S(1)} %copy-done.3), custom_call_target="tpu_custom_call" | custom-call | tf_op jit(solution)/shard_map/pallas_call | solution.py:484
  104.1 0.7 copy.8
  104.9 0.5 copy.9
Async XLA Ops:
  0.6 0.9 copy-start
  1.5 0.9 copy-start.1
  2.4 0.7 copy-start.2
  3.1 0.7 copy-start.3
where the time goes:
time: 106 us; the launch traced here: 105 us
  Pallas kernels  100 us (94%)
  local copies, waits for them, and re-layouts  4.37 us (4%)
    pallas_call x1, Pallas kernels, step(): pl.pallas_call(functools.partial(kernel, sizes), out_shape=(jax.ShapeDtyp...  100 us
    unnamed x10, local copies, waits for them, and re-layouts  4.37 us

commit v1 on v0

--- a/solution.py
+++ b/solution.py
@@ -30,10 +30,10 @@
 
 def kernel(
     sizes,
-    src_hbm, tgt_hbm, kern, smo,
-    disp_hbm, mis,
-    a_ref, b_ref, f, zp, zb, t, tz, w, tots, totb, out,
-    xb, yb, pz, zs, t2, tz2,
+    src_hbm, tgt_hbm, kern_hbm, smo_hbm,
+    out, mis,
+    a_ref, b_ref, kern, smo, f, zp, zb, t, tz, w, tots, totb, inv,
+    xb, yb, pz, zs, tz2,
     send, recv, xsend, xrecv, ysend, yrecv, lsend, lrecv, loc,
 ):
     nx, ny, nz = sizes
@@ -47,6 +47,8 @@
     loads = [
         pltpu.make_async_copy(src_hbm, a_ref, loc.at[0]),
         pltpu.make_async_copy(tgt_hbm, b_ref, loc.at[1]),
+        pltpu.make_async_copy(kern_hbm, kern, loc.at[2]),
+        pltpu.make_async_copy(smo_hbm, smo, loc.at[3]),
     ]
     for c in loads:
         c.start()
@@ -82,28 +84,14 @@
                     zb[p, q, e, pl.ds(8 * j, 8), :] = zero
 
     barrier = pltpu.get_barrier_semaphore()
-    expected = sum(n - 1 for _, n in pos.values())
-    for axis, (m, n) in pos.items():
-        for j in range(1, n):
-            pl.semaphore_signal(
-                barrier, 1, device_id={axis: lax.rem(m + j, n)}, device_id_type=MESH
-            )
+    expected = 0
     for d in DIRS:
-        if sum(abs(c) for c in d) > 1:
-            there = has(d)
-            expected = expected + jnp.where(there, 1, 0)
-
-            @pl.when(there)
-            def _():
-                pl.semaphore_signal(barrier, 1, device_id=peer(d), device_id_type=MESH)
-
-    k = [kern[i] for i in range(R + 1)]
-    norm = smo[0]
-    tail = smo[1]
-    for i in range(2, S + 1):
-        tail = tail + smo[i]
-    norm = jnp.full((8, BZ), norm + 2.0 * tail, F32)
-    s = [jnp.full((8, BZ), smo[i], F32) / norm for i in range(S + 1)]
+        there = has(d)
+        expected = expected + jnp.where(there, 1, 0)
+
+        @pl.when(there)
+        def _():
+            pl.semaphore_signal(barrier, 1, device_id=peer(d), device_id_type=MESH)
 
     for c in range(3):
         for i in range(BX):
@@ -116,20 +104,30 @@
             for j in range(TY + 2):
                 zs[c, q, pl.ds(8 * j, 8), :] = zero
 
+    for c in loads[2:]:
+        c.wait()
+    k = [kern[i] for i in range(R + 1)]
+    norm = smo[0]
+    tail = smo[1]
+    for i in range(2, S + 1):
+        tail = tail + smo[i]
+    norm = jnp.full((8, BZ), norm + 2.0 * tail, F32)
+    s = [jnp.full((8, BZ), smo[i], F32) / norm for i in range(S + 1)]
+
     def copy(p, d):
         i = DIRS.index(d)
         dx, dy, dz = d
         if dz == 0:
             xs = {1: pl.ds(BX, R), -1: pl.ds(R, R), 0: pl.ds(R, BX)}[dx]
             xd = {1: pl.ds(0, R), -1: pl.ds(R + BX, R), 0: pl.ds(R, BX)}[dx]
-            ys = {1: pl.ds(BY, 8), -1: pl.ds(8, 8), 0: pl.ds(8, BY)}[dy]
-            yd = {1: pl.ds(0, 8), -1: pl.ds(BY + 8, 8), 0: pl.ds(8, BY)}[dy]
+            ys = {1: pl.ds(BY + 8 - R, R), -1: pl.ds(8, R), 0: pl.ds(8, BY)}[dy]
+            yd = {1: pl.ds(8 - R, R), -1: pl.ds(BY + 8, R), 0: pl.ds(8, BY)}[dy]
             source, target = f.at[p, xs, ys], f.at[p, xd, yd]
         else:
             side = 0 if dz > 0 else 1
-            rows = {1: pl.ds(8, 8), -1: pl.ds(0, 8), 0: pl.ds(0, 16)}[dy]
-            lands = {1: pl.ds(0, 8), -1: pl.ds(24, 8), 0: pl.ds(8, 16)}[dy]
-            source, target = zp.at[p, rows], zb.at[p, side, 1 - dx, lands]
+            rows = {1: pl.ds(8, 8), -1: pl.ds(0, 8), 0: pl.ds(0, 16)}[dx]
+            lands = {1: pl.ds(0, 8), -1: pl.ds(24, 8), 0: pl.ds(8, 16)}[dx]
+            source, target = zp.at[p, rows], zb.at[p, side, 1 - dy, lands]
         return pltpu.make_async_remote_copy(
             src_ref=source, dst_ref=target, send_sem=send.at[p, i],
             recv_sem=recv.at[p, i], device_id=peer(d), device_id_type=MESH,
@@ -205,18 +203,18 @@
     def packed_in(p):
         left = (lane % 8) < R
         tiles = []
-        for e in range(4):
-            rows = pl.ds(8 * e, 8)
-            face = jnp.where(left, zb[p, 0, 1, rows, :], zb[p, 1, 1, rows, :])
-            low = jnp.where(left, zb[p, 0, 0, rows, :], zb[p, 1, 0, rows, :])
-            high = jnp.where(left, zb[p, 0, 2, rows, :], zb[p, 1, 2, rows, :])
-            edge = jnp.where((lane % 64) >= 32, low, high)
-            for h in {0: (1,), 1: (0, 1), 2: (0, 1), 3: (0,)}[e]:
+        for e, hs in enumerate(((TY - 1,), range(TY), (0,))):
+            parts = [
+                jnp.where(left, zb[p, 0, e, pl.ds(8 * g, 8), :], zb[p, 1, e, pl.ds(8 * g, 8), :])
+                for g in range(4)
+            ]
+            for h in hs:
+                moved = [roll(parts[g], 32 * (g - h)) for g in range(4)]
                 tiles.append(
                     jnp.where(
-                        (lane >= 32) & (lane < 96),
-                        roll(face, 32 - 64 * h),
-                        roll(edge, 96 - 64 * h),
+                        lane < 64,
+                        jnp.where(lane < 32, moved[0], moved[1]),
+                        jnp.where(lane < 96, moved[2], moved[3]),
                     )
                 )
         return tiles
@@ -242,8 +240,8 @@
         return {}
 
     def pack(acc, v, i, j):
-        e, h = divmod(j, 2)
-        at = 64 * h + 8 * i
+        e, g = divmod(i, 4)
+        at = 32 * j + 8 * g
         moved = roll(v, at + 4)
         acc[e] = moved if e not in acc else jnp.where((lane >= at) & (lane < at + 8), moved, acc[e])
 
@@ -277,7 +275,7 @@
     sum_y = [ones_sum(sub + (my * BY + 8 * j), ny * BY) * sum_z for j in range(TY)]
     sum_x = [ones_sum(mx * BX + i, nx * BX) for i in range(BX)]
 
-    for c in loads:
+    for c in loads[:2]:
         c.wait()
     acc = pack_init()
     total_a, total_b = zero, zero
@@ -290,11 +288,11 @@
             f[1, R + i, pl.ds(8 + 8 * j, 8), :] = jnp.ones((8, BZ), F32)
             put(0, i, j, a / (sum_x[i] * sum_y[j]), acc)
     flush(0, acc)
-    tots[0, 0, pl.ds(0, 8), :] = total_a
-    tots[0, 0, pl.ds(8, 8), :] = total_b
+    total_a = jnp.broadcast_to(jnp.sum(total_a, axis=0, keepdims=True), (8, BZ))
+    total_b = jnp.broadcast_to(jnp.sum(total_b, axis=0, keepdims=True), (8, BZ))
+    tots[0, 0] = jnp.where(sub == 0, total_a, jnp.where(sub == 1, total_b, zero))
     pl.semaphore_wait(barrier, expected)
     start(0)
-    line("gx", 0, True)
 
     def v_step(n):
         arrived(0, DIRS)
@@ -325,17 +323,22 @@
     def iteration(n, carry):
         v_step(n)
 
-        @pl.when(n == 1)
+        @pl.when(n == 3)
+        def _():
+            line("gx", 0, True)
+
+        @pl.when(n == 4)
+        def _():
+            line_end("gy", 0)
+            line("gz", 0, True)
+
+        u_step()
+
+        @pl.when(n == 3)
         def _():
             line_end("gx", 0)
             line("gy", 0, True)
 
-        @pl.when(n == 3)
-        def _():
-            line_end("gy", 0)
-            line("gz", 0, True)
-
-        u_step()
         return carry
 
     lax.fori_loop(0, ITERS - 1, iteration, 0)
@@ -343,11 +346,11 @@
 
     line_end("gz", 0)
 
-    def everything(v):
+    def everything(row):
+        v = jnp.where(sub == row, tots[0, 3], zero)
         return jnp.full((8, BZ), cells, F32) / jnp.full((8, BZ), jnp.sum(v), F32)
 
-    alpha = everything(tots[0, 3, pl.ds(0, 8), :])
-    beta = everything(tots[0, 3, pl.ds(8, 8), :])
+    alpha, beta = everything(0), everything(1)
     rows = zero
     for n in range(ITERS):
         part = zero
@@ -357,30 +360,8 @@
                 part = part + jnp.abs(alpha * w[n, i, at, :] - beta * b_ref[i, at, :])
         part = jnp.broadcast_to(jnp.sum(part, axis=0, keepdims=True), (8, BZ))
         rows = jnp.where(sub == n, part, rows)
-    tots[1, 0, pl.ds(0, 8), :] = rows
-    tots[1, 0, pl.ds(8, 8), :] = zero
+    tots[1, 0] = rows
     line("gx", 1, True)
-
-    arrived(1, DIRS)
-    x_pass(1, t, [symmetric, slope])
-    x_pass_packed(1, tz, [symmetric, slope])
-    for j in range(TY):
-        at = pl.ds(8 + 8 * j, 8)
-        halos = [
-            symmetric(k, y_at(tz.at[0], j)),
-            slope(k, y_at(tz.at[0], j)),
-            symmetric(k, y_at(tz.at[1], j)),
-        ]
-        for i in range(BX):
-            by = -(8 * (i + R) + 4)
-            kk, kg = symmetric(k, y_at(t.at[0, i], j)), slope(k, y_at(t.at[0, i], j))
-            gk = symmetric(k, y_at(t.at[1, i], j))
-            kvol, znum = along_z(kk, roll(halos[0], by), k, [symmetric, slope])
-            ynum = along_z(kg, roll(halos[1], by), k, [symmetric])[0]
-            xnum = along_z(gk, roll(halos[2], by), k, [symmetric])[0]
-            inverse = 1.0 / kvol
-            for c, num in enumerate((xnum, ynum, znum)):
-                xb[c, BX + i, pl.ds(8 * j, 8), :] = num * inverse
 
     def x_copy(c, d):
         lands = 0 if d > 0 else 2 * BX
@@ -408,46 +389,46 @@
             recv_sem=yrecv.at[c, i], device_id=peer(d), device_id_type=MESH,
         )
 
-    for c in range(3):
+    def x_start(c):
         for d in (-1, 1):
             @pl.when(conds[0][d])
             def _():
                 x_copy(c, d).start()
-    sent(1)
-    line_end("gx", 1)
-    line("gy", 1, True)
-
-    stores = [pltpu.make_async_copy(out.at[c], disp_hbm.at[c], loc.at[2 + c]) for c in range(3)]
-
-    for c in range(3):
+
+    def x_arrived(c):
         for d in (-1, 1):
             @pl.when(conds[0][-d])
             def _():
                 x_copy(c, d).wait_recv()
+
+    def y_start(c):
+        for d in YZ:
+            @pl.when(has(d))
+            def _():
+                y_copy(c, d).start()
+
+    def y_arrived(c):
+        for d in YZ:
+            @pl.when(has(neg(d)))
+            def _():
+                y_copy(c, d).wait_recv()
+
+    def y_put(c, value):
         for j in range(TY):
-            at = pl.ds(8 * j, 8)
             packed = None
             for i in range(BX):
-                v = symmetric(s, lambda d: xb[c, BX + i + d, at, :])
+                v = value(i, j)
                 yb[c, i, pl.ds(8 + 8 * j, 8), :] = v
                 moved = roll(v, 16 * i + 8)
                 packed = moved if packed is None else jnp.where(
                     (lane >= 16 * i) & (lane < 16 * i + 16), moved, packed
                 )
-            pz[c, at, :] = packed
-        for d in YZ:
-            @pl.when(has(d))
-            def _():
-                y_copy(c, d).start()
-        if c == 0:
-            line_end("gy", 1)
-            line("gz", 1, True)
-
-    for c in range(3):
-        for d in YZ:
-            @pl.when(has(neg(d)))
-            def _():
-                y_copy(c, d).wait_recv()
+            pz[c, pl.ds(8 * j, 8), :] = packed
+
+    def smooth_x(c, i, j):
+        return symmetric(s, lambda d: xb[c, BX + i + d, pl.ds(8 * j, 8), :])
+
+    def smooth_yz(c, put_value):
         for j in range(TY + 2):
             at = pl.ds(8 * j, 8)
             tz2[at, :] = jnp.where((lane % 16) < S, zs[c, 0, at, :], zs[c, 1, at, :])
@@ -455,13 +436,75 @@
             halos = symmetric(s, y_at(tz2, j))
             for i in range(BX):
                 own = symmetric(s, y_at(yb.at[c, i], j))
-                out[c, i, pl.ds(8 * j, 8), :] = along_z(
-                    own, roll(halos, -(16 * i + 8)), s, [symmetric]
-                )[0]
-        stores[c].start()
+                put_value(i, j, along_z(own, roll(halos, -(16 * i + 8)), s, [symmetric])[0])
+
+    def at_z(i, halos):
+        return roll(halos, -(8 * (i + R) + 4))
+
+    arrived(1, DIRS)
+    x_pass(1, t, [symmetric, slope])
+    x_pass_packed(1, tz, [symmetric, slope])
+    for j in range(TY):
+        halos = symmetric(k, y_at(tz.at[0], j))
+        for i in range(BX):
+            kk = symmetric(k, y_at(t.at[0, i], j))
+            kvol, znum = along_z(kk, at_z(i, halos), k, [symmetric, slope])
+            inverse = 1.0 / kvol
+            inv[i, pl.ds(8 * j, 8), :] = inverse
+            xb[2, BX + i, pl.ds(8 * j, 8), :] = znum * inverse
+    x_start(2)
+
+    halos = [slope(k, y_at(tz.at[0], j)) for j in range(TY)]
+
+    def raw_y(i, j):
+        kg = slope(k, y_at(t.at[0, i], j))
+        return along_z(kg, at_z(i, halos[j]), k, [symmetric])[0] * inv[i, pl.ds(8 * j, 8), :]
+
+    y_put(1, raw_y)
+    y_start(1)
+
+    for j in range(TY):
+        halos = symmetric(k, y_at(tz.at[1], j))
+        for i in range(BX):
+            gk = symmetric(k, y_at(t.at[1, i], j))
+            xnum = along_z(gk, at_z(i, halos), k, [symmetric])[0]
+            xb[0, BX + i, pl.ds(8 * j, 8), :] = xnum * inv[i, pl.ds(8 * j, 8), :]
+    x_start(0)
+    sent(1)
+    line_end("gx", 1)
+    line("gy", 1, True)
+
+    y_arrived(1)
+
+    def to_x(i, j, v):
+        xb[1, BX + i, pl.ds(8 * j, 8), :] = v
+
+    smooth_yz(1, to_x)
+    x_start(1)
+    line_end("gy", 1)
+    line("gz", 1, True)
+
+    def to_out(c):
+        def put_value(i, j, v):
+            out[c, i, pl.ds(8 * j, 8), :] = v
+
+        return put_value
+
+    for c in (2, 0):
+        x_arrived(c)
+        y_put(c, functools.partial(smooth_x, c))
+        y_start(c)
+    y_arrived(2)
+    smooth_yz(2, to_out(2))
+    x_arrived(1)
+    for j in range(TY):
+        for i in range(BX):
+            to_out(1)(i, j, smooth_x(1, i, j))
+    y_arrived(0)
+    smooth_yz(0, to_out(0))
 
     line_end("gz", 1)
-    done = tots[1, 3, pl.ds(0, 8), :]
+    done = tots[1, 3]
     for n in range(ITERS):
         mis[n] = jnp.sum(jnp.where(sub == n, done, 0.0)) / cells
     for c in range(3):
@@ -473,7 +516,6 @@
             @pl.when(has(d))
             def _():
                 y_copy(c, d).wait_send()
-        stores[c].wait()
 
 
 def solution(mesh):
@@ -487,33 +529,29 @@
                 jax.ShapeDtypeStruct((3, BX, BY, BZ), F32),
                 jax.ShapeDtypeStruct((ITERS,), F32),
             ),
-            in_specs=[
-                pl.BlockSpec(memory_space=pl.ANY),
-                pl.BlockSpec(memory_space=pl.ANY),
-                pl.BlockSpec(memory_space=pltpu.SMEM),
-                pl.BlockSpec(memory_space=pltpu.SMEM),
-            ],
+            in_specs=[pl.BlockSpec(memory_space=pltpu.HBM)] * 4,
             out_specs=(
-                pl.BlockSpec(memory_space=pl.ANY),
+                pl.BlockSpec(memory_space=pltpu.VMEM),
                 pl.BlockSpec(memory_space=pltpu.SMEM),
             ),
             scratch_shapes=[
                 pltpu.VMEM((BX, BY, BZ), F32),
                 pltpu.VMEM((BX, BY, BZ), F32),
+                pltpu.SMEM((R + 1,), F32),
+                pltpu.SMEM((S + 1,), F32),
                 pltpu.VMEM((2, BX + 2 * R, BY + 16, BZ), F32),
                 pltpu.VMEM((2, 16, BZ), F32),
                 pltpu.VMEM((2, 2, 3, 32, BZ), F32),
                 pltpu.VMEM((2, BX, BY + 16, BZ), F32),
                 pltpu.VMEM((2, BY + 16, BZ), F32),
                 pltpu.VMEM((ITERS, BX, BY, BZ), F32),
-                pltpu.VMEM((2, 4, 16, BZ), F32),
-                pltpu.VMEM((2, peers, 16, BZ), F32),
-                pltpu.VMEM((3, BX, BY, BZ), F32),
+                pltpu.VMEM((2, 4, 8, BZ), F32),
+                pltpu.VMEM((2, peers, 8, BZ), F32),
+                pltpu.VMEM((BX, BY, BZ), F32),
                 pltpu.VMEM((3, 3 * BX, BY, BZ), F32),
                 pltpu.VMEM((3, BX, BY + 16, BZ), F32),
                 pltpu.VMEM((3, BY, BZ), F32),
                 pltpu.VMEM((3, 2, BY + 16, BZ), F32),
-                pltpu.VMEM((8, BZ), F32),
                 pltpu.VMEM((BY + 16, BZ), F32),
                 pltpu.SemaphoreType.DMA((2, 26)),
                 pltpu.SemaphoreType.DMA((2, 26)),
@@ -523,10 +561,10 @@
                 pltpu.SemaphoreType.DMA((3, 8)),
                 pltpu.SemaphoreType.DMA((2, peers)),
                 pltpu.SemaphoreType.DMA((2, peers)),
-                pltpu.SemaphoreType.DMA((5,)),
+                pltpu.SemaphoreType.DMA((4,)),
             ],
             compiler_params=pltpu.CompilerParams(
-                collective_id=0, has_side_effects=True, vmem_limit_bytes=32 * 1024 * 1024
+                collective_id=0, has_side_effects=True, vmem_limit_bytes=67043328
             ),
         )(source, target, kernel_half, smooth_half)
 

time: 106 us -> 92.1 us (0.87)
  Pallas kernels: 100 us -> 89.1 us
  local copies, waits for them, and re-layouts: 4.37 us -> 2.28 us
    pallas_call x1, Pallas kernels: 100 us -> 89.1 us  [step(): pl.pallas_call(functools.partial(kernel, sizes), out_shape=(jax.ShapeDtyp...]
    unnamed x10 -> x4, local copies, waits for them, and re-layouts: 4.37 us -> 2.28 us
where the time goes in v1:
time: 92.1 us; the launch traced here: 92 us
  Pallas kernels  89.1 us (97%)
  local copies, waits for them, and re-layouts  2.28 us (2%)
    pallas_call x1, Pallas kernels, step(): pl.pallas_call(functools.partial(kernel, sizes), out_shape=(jax.ShapeDtyp...  89.1 us
    unnamed x4, local copies, waits for them, and re-layouts  2.28 us

profile of v1, /device:TPU:1, one launch (start us, length us, event | category | flops | bytes accessed | tf_op | source)
XLA Modules:
  0.0 92.0 jit_solution(6903651643420962688)
XLA Ops:
  0.6 89.1 %shard_map.59 = (f32[3,8,32,128]{3,2,1,0:T(8,128)}, f32[6]{0:T(128)}) custom-call(f32[8,32,128]{2,1,0:T(8,128)} %src_hbm.1, f32[8,32,128]{2,1,0:T(8,128)} %tgt_hbm.1, f32[5]{0:T(128)} %kern_hbm.1, f32[9]{0:T(128)} %smo_hbm.1), custom_call_target="tpu_custom_call" | custom-call | tf_op jit(solution)/shard_map/pallas_call | solution.py:526
  89.7 0.0 copy-start
  89.7 1.8 %copy.8 = f32[3,8,32,128]{3,2,1,0:T(8,128)} copy(f32[3,8,32,128]{3,2,1,0:T(8,128)} %get-tuple-element.4) | data formatting | bytes 786432
  91.5 0.0 copy-done
  91.5 0.5 copy.9
Async XLA Ops:
  89.7 1.8 %copy-start = (f32[6]{0:T(128)S(1)}, f32[6]{0:T(128)}, u32[]{:S(2)}) copy-start(f32[6]{0:T(128)} %get-tuple-element.5) | copy-start | bytes 76

commit v2 on v1

--- a/solution.py
+++ b/solution.py
@@ -26,6 +26,7 @@
     key=lambda d: (-sum(abs(c) for c in d), abs(d[0]), abs(d[1]), d),
 )
 YZ = [d for d in DIRS if d[0] == 0]
+SMALL = [d for d in DIRS if d[1:] != (0, 0)]
 
 
 def kernel(
@@ -34,7 +35,7 @@
     out, mis,
     a_ref, b_ref, kern, smo, f, zp, zb, t, tz, w, tots, totb, inv,
     xb, yb, pz, zs, tz2,
-    send, recv, xsend, xrecv, ysend, yrecv, lsend, lrecv, loc,
+    send, recv, fsend, frecv, xsend, xrecv, ysend, yrecv, lsend, lrecv, loc,
 ):
     nx, ny, nz = sizes
     cells = float(nx * ny * nz * BX * BY * BZ)
@@ -75,7 +76,7 @@
         return tuple(-c for c in d)
 
     for p in range(2):
-        for i in range(2 * R + BX):
+        for i in range(3 * R + BX):
             for j in range(TY + 2):
                 f[p, i, pl.ds(8 * j, 8), :] = zero
         for q in range(2):
@@ -133,17 +134,49 @@
             recv_sem=recv.at[p, i], device_id=peer(d), device_id_type=MESH,
         )
 
+    other = mz + 1 - 2 * lax.rem(mz, 2)
+
+    def face(p, d, j):
+        ok = conds[0][d]
+        near, far = (R + BX, 0) if d < 0 else (0, R + BX)
+        e = jnp.where(ok, near, far)
+        source = jnp.where(ok, BX if d > 0 else R, 2 * R + BX)
+        side = jnp.where(ok, 0 if d > 0 else 1, 1 if d > 0 else 0)
+        rows = pl.ds(8 + 8 * j, 8)
+        return pltpu.make_async_remote_copy(
+            src_ref=f.at[p, pl.ds(source, R), rows], dst_ref=f.at[p, pl.ds(e, R), rows],
+            send_sem=fsend.at[p, 0 if d > 0 else 1, j], recv_sem=frecv.at[p, side, j],
+            device_id={"gx": jnp.where(ok, mx + d, mx), "gz": jnp.where(ok, mz, other)},
+            device_id_type=MESH,
+        )
+
+    def face_start(p, j):
+        for d in (1, -1):
+            face(p, d, j).start()
+
+    def face_arrived(p, j):
+        rows = pl.ds(8 + 8 * j, 8)
+        for side, at in ((0, 0), (1, R + BX)):
+            pltpu.make_async_remote_copy(
+                src_ref=f.at[p, pl.ds(BX, R), rows], dst_ref=f.at[p, pl.ds(at, R), rows],
+                send_sem=fsend.at[p, side, j], recv_sem=frecv.at[p, side, j],
+                device_id={"gz": other}, device_id_type=MESH,
+            ).wait_recv()
+
     def start(p):
-        for d in DIRS:
+        for d in SMALL:
             @pl.when(has(d))
             def _():
                 copy(p, d).start()
 
     def sent(p):
-        for d in DIRS:
+        for d in SMALL:
             @pl.when(has(d))
             def _():
                 copy(p, d).wait_send()
+        for j in range(TY):
+            for d in (1, -1):
+                face(p, d, j).wait_send()
 
     def arrived(p, dirs):
         for d in dirs:
@@ -219,13 +252,12 @@
                 )
         return tiles
 
-    def x_pass(p, dst, passes):
-        for j in range(TY + 2):
-            rows = pl.ds(8 * j, 8)
-            col = [f[p, i, rows, :] for i in range(2 * R + BX)]
-            for i in range(BX):
-                for n, q in enumerate(passes):
-                    dst[n, i, rows, :] = q(k, lambda d: col[i + R + d])
+    def x_tile(p, j, dst, passes):
+        rows = pl.ds(8 * j, 8)
+        col = [f[p, i, rows, :] for i in range(2 * R + BX)]
+        for i in range(BX):
+            for n, q in enumerate(passes):
+                dst[n, i, rows, :] = q(k, lambda d: col[i + R + d])
 
     def x_pass_packed(p, dst, passes):
         for j, z in enumerate(packed_in(p)):
@@ -245,15 +277,26 @@
         moved = roll(v, at + 4)
         acc[e] = moved if e not in acc else jnp.where((lane >= at) & (lane < at + 8), moved, acc[e])
 
-    def apply(p, use):
-        x_pass(p, t, [symmetric])
+    def apply(p, use, after):
+        arrived(p, SMALL)
+        for j in (0, TY + 1):
+            x_tile(p, j, t, [symmetric])
         x_pass_packed(p, tz, [symmetric])
-        for j in range(TY):
-            halos = symmetric(k, y_at(tz.at[0], j))
+        halos = [symmetric(k, y_at(tz.at[0], j)) for j in range(TY)]
+
+        def row(j):
             for i in range(BX):
                 own = symmetric(k, y_at(t.at[0, i], j))
-                halo = roll(halos, -(8 * (i + R) + 4))
+                halo = roll(halos[j], -(8 * (i + R) + 4))
                 use(i, j, along_z(own, halo, k, [symmetric])[0])
+            after(j)
+
+        for j in range(TY):
+            face_arrived(p, j)
+            x_tile(p, j + 1, t, [symmetric])
+            if j:
+                row(j - 1)
+        row(TY - 1)
 
     def put(p, i, j, v, acc):
         f[p, R + i, pl.ds(8 + 8 * j, 8), :] = v
@@ -293,9 +336,10 @@
     tots[0, 0] = jnp.where(sub == 0, total_a, jnp.where(sub == 1, total_b, zero))
     pl.semaphore_wait(barrier, expected)
     start(0)
+    for j in range(TY):
+        face_start(0, j)
 
     def v_step(n):
-        arrived(0, DIRS)
         acc = pack_init()
 
         def use(i, j, ku):
@@ -303,19 +347,18 @@
             w[n, i, pl.ds(8 * j, 8), :] = v * ku
             put(1, i, j, b_ref[i, pl.ds(8 * j, 8), :] / ku, acc)
 
-        apply(0, use)
+        apply(0, use, lambda j: face_start(1, j))
         flush(1, acc)
         start(1)
         sent(0)
 
     def u_step():
-        arrived(1, DIRS)
         acc = pack_init()
 
         def use(i, j, kv):
             put(0, i, j, a_ref[i, pl.ds(8 * j, 8), :] / kv, acc)
 
-        apply(1, use)
+        apply(1, use, lambda j: face_start(0, j))
         flush(0, acc)
         start(0)
         sent(1)
@@ -441,8 +484,11 @@
     def at_z(i, halos):
         return roll(halos, -(8 * (i + R) + 4))
 
-    arrived(1, DIRS)
-    x_pass(1, t, [symmetric, slope])
+    arrived(1, SMALL)
+    for j in range(TY):
+        face_arrived(1, j)
+    for j in range(TY + 2):
+        x_tile(1, j, t, [symmetric, slope])
     x_pass_packed(1, tz, [symmetric, slope])
     for j in range(TY):
         halos = symmetric(k, y_at(tz.at[0], j))
@@ -539,7 +585,7 @@
                 pltpu.VMEM((BX, BY, BZ), F32),
                 pltpu.SMEM((R + 1,), F32),
                 pltpu.SMEM((S + 1,), F32),
-                pltpu.VMEM((2, BX + 2 * R, BY + 16, BZ), F32),
+                pltpu.VMEM((2, BX + 3 * R, BY + 16, BZ), F32),
                 pltpu.VMEM((2, 16, BZ), F32),
                 pltpu.VMEM((2, 2, 3, 32, BZ), F32),
                 pltpu.VMEM((2, BX, BY + 16, BZ), F32),
@@ -555,6 +601,8 @@
                 pltpu.VMEM((BY + 16, BZ), F32),
                 pltpu.SemaphoreType.DMA((2, 26)),
                 pltpu.SemaphoreType.DMA((2, 26)),
+                pltpu.SemaphoreType.DMA((2, 2, TY)),
+                pltpu.SemaphoreType.DMA((2, 2, TY)),
                 pltpu.SemaphoreType.DMA((3, 2)),
                 pltpu.SemaphoreType.DMA((3, 2)),
                 pltpu.SemaphoreType.DMA((3, 8)),

time: 92.1 us -> 98.8 us (1.073)
  Pallas kernels: 89.1 us -> 95.8 us
    pallas_call x1, Pallas kernels: 89.1 us -> 95.8 us  [step(): pl.pallas_call(functools.partial(kernel, sizes), out_shape=(jax.ShapeDtyp...]
where the time goes in v2:
time: 98.8 us; the launch traced here: 98.7 us
  Pallas kernels  95.8 us (97%)
  local copies, waits for them, and re-layouts  2.28 us (2%)
    pallas_call x1, Pallas kernels, step(): pl.pallas_call(functools.partial(kernel, sizes), out_shape=(jax.ShapeDtyp...  95.8 us
    unnamed x4, local copies, waits for them, and re-layouts  2.28 us

profile of v2, /device:TPU:1, one launch (start us, length us, event | category | flops | bytes accessed | tf_op | source)
XLA Modules:
  0.0 98.7 jit_solution(2822126962218244708)
XLA Ops:
  0.6 95.8 %shard_map.59 = (f32[3,8,32,128]{3,2,1,0:T(8,128)}, f32[6]{0:T(128)}) custom-call(f32[8,32,128]{2,1,0:T(8,128)} %src_hbm.1, f32[8,32,128]{2,1,0:T(8,128)} %tgt_hbm.1, f32[5]{0:T(128)} %kern_hbm.1, f32[9]{0:T(128)} %smo_hbm.1), custom_call_target="tpu_custom_call" | custom-call | tf_op jit(solution)/shard_map/pallas_call | solution.py:572
  96.4 0.0 copy-start
  96.4 1.8 %copy.8 = f32[3,8,32,128]{3,2,1,0:T(8,128)} copy(f32[3,8,32,128]{3,2,1,0:T(8,128)} %get-tuple-element.4) | data formatting | bytes 786432
  98.2 0.0 copy-done
  98.2 0.5 copy.9
Async XLA Ops:
  96.4 1.8 %copy-start = (f32[6]{0:T(128)S(1)}, f32[6]{0:T(128)}, u32[]{:S(2)}) copy-start(f32[6]{0:T(128)} %get-tuple-element.5) | copy-start | bytes 76

commit v3 on v1

--- a/solution.py
+++ b/solution.py
@@ -23,7 +23,7 @@
         for dz in (-1, 0, 1)
         if (dx, dy, dz) != (0, 0, 0)
     ],
-    key=lambda d: (-sum(abs(c) for c in d), abs(d[0]), abs(d[1]), d),
+    key=lambda d: (d[1:] == (0, 0), -sum(abs(c) for c in d), -abs(d[0]), -abs(d[2]), d),
 )
 YZ = [d for d in DIRS if d[0] == 0]
 
@@ -31,8 +31,8 @@
 def kernel(
     sizes,
     src_hbm, tgt_hbm, kern_hbm, smo_hbm,
-    out, mis,
-    a_ref, b_ref, kern, smo, f, zp, zb, t, tz, w, tots, totb, inv,
+    disp_hbm, mis,
+    a_ref, b_ref, kern, smo, f, zp, zb, t, tz, w, tots, totb, inv, out,
     xb, yb, pz, zs, tz2,
     send, recv, xsend, xrecv, ysend, yrecv, lsend, lrecv, loc,
 ):
@@ -81,7 +81,7 @@
         for q in range(2):
             for e in range(3):
                 for j in range(4):
-                    zb[p, q, e, pl.ds(8 * j, 8), :] = zero
+                    zb[p, q, e, j] = zero
 
     barrier = pltpu.get_barrier_semaphore()
     expected = 0
@@ -125,9 +125,10 @@
             source, target = f.at[p, xs, ys], f.at[p, xd, yd]
         else:
             side = 0 if dz > 0 else 1
-            rows = {1: pl.ds(8, 8), -1: pl.ds(0, 8), 0: pl.ds(0, 16)}[dx]
-            lands = {1: pl.ds(0, 8), -1: pl.ds(24, 8), 0: pl.ds(8, 16)}[dx]
-            source, target = zp.at[p, rows], zb.at[p, side, 1 - dy, lands]
+            layers = {1: pl.ds(1, 1), -1: pl.ds(0, 1), 0: pl.ds(0, 2)}[dx]
+            lands = {1: pl.ds(0, 1), -1: pl.ds(3, 1), 0: pl.ds(1, 2)}[dx]
+            rows = {1: pl.ds(8 - R, R), -1: pl.ds(0, R), 0: pl.ds(0, 8)}[dy]
+            source, target = zp.at[p, layers, rows], zb.at[p, side, 1 - dy, lands, rows]
         return pltpu.make_async_remote_copy(
             src_ref=source, dst_ref=target, send_sem=send.at[p, i],
             recv_sem=recv.at[p, i], device_id=peer(d), device_id_type=MESH,
@@ -205,7 +206,7 @@
         tiles = []
         for e, hs in enumerate(((TY - 1,), range(TY), (0,))):
             parts = [
-                jnp.where(left, zb[p, 0, e, pl.ds(8 * g, 8), :], zb[p, 1, e, pl.ds(8 * g, 8), :])
+                jnp.where(left, zb[p, 0, e, g], zb[p, 1, e, g])
                 for g in range(4)
             ]
             for h in hs:
@@ -261,7 +262,7 @@
 
     def flush(p, acc):
         for e, v in acc.items():
-            zp[p, pl.ds(8 * e, 8), :] = v
+            zp[p, e] = v
 
     def ones_sum(index, n):
         acc = None
@@ -494,14 +495,18 @@
         x_arrived(c)
         y_put(c, functools.partial(smooth_x, c))
         y_start(c)
+    stores = [pltpu.make_async_copy(out.at[c], disp_hbm.at[c], loc.at[4 + c]) for c in range(3)]
     y_arrived(2)
     smooth_yz(2, to_out(2))
+    stores[2].start()
     x_arrived(1)
     for j in range(TY):
         for i in range(BX):
             to_out(1)(i, j, smooth_x(1, i, j))
+    stores[1].start()
     y_arrived(0)
     smooth_yz(0, to_out(0))
+    stores[0].start()
 
     line_end("gz", 1)
     done = tots[1, 3]
@@ -516,6 +521,7 @@
             @pl.when(has(d))
             def _():
                 y_copy(c, d).wait_send()
+        stores[c].wait()
 
 
 def solution(mesh):
@@ -531,7 +537,7 @@
             ),
             in_specs=[pl.BlockSpec(memory_space=pltpu.HBM)] * 4,
             out_specs=(
-                pl.BlockSpec(memory_space=pltpu.VMEM),
+                pl.BlockSpec(memory_space=pltpu.HBM),
                 pl.BlockSpec(memory_space=pltpu.SMEM),
             ),
             scratch_shapes=[
@@ -540,14 +546,15 @@
                 pltpu.SMEM((R + 1,), F32),
                 pltpu.SMEM((S + 1,), F32),
                 pltpu.VMEM((2, BX + 2 * R, BY + 16, BZ), F32),
-                pltpu.VMEM((2, 16, BZ), F32),
-                pltpu.VMEM((2, 2, 3, 32, BZ), F32),
+                pltpu.VMEM((2, 2, 8, BZ), F32),
+                pltpu.VMEM((2, 2, 3, 4, 8, BZ), F32),
                 pltpu.VMEM((2, BX, BY + 16, BZ), F32),
                 pltpu.VMEM((2, BY + 16, BZ), F32),
                 pltpu.VMEM((ITERS, BX, BY, BZ), F32),
                 pltpu.VMEM((2, 4, 8, BZ), F32),
                 pltpu.VMEM((2, peers, 8, BZ), F32),
                 pltpu.VMEM((BX, BY, BZ), F32),
+                pltpu.VMEM((3, BX, BY, BZ), F32),
                 pltpu.VMEM((3, 3 * BX, BY, BZ), F32),
                 pltpu.VMEM((3, BX, BY + 16, BZ), F32),
                 pltpu.VMEM((3, BY, BZ), F32),
@@ -561,7 +568,7 @@
                 pltpu.SemaphoreType.DMA((3, 8)),
                 pltpu.SemaphoreType.DMA((2, peers)),
                 pltpu.SemaphoreType.DMA((2, peers)),
-                pltpu.SemaphoreType.DMA((4,)),
+                pltpu.SemaphoreType.DMA((7,)),
             ],
             compiler_params=pltpu.CompilerParams(
                 collective_id=0, has_side_effects=True, vmem_limit_bytes=67043328

time: 92.1 us -> 91.1 us (0.989)
  Pallas kernels: 89.1 us -> 88.1 us
    pallas_call x1, Pallas kernels: 89.1 us -> 88.1 us  [step(): pl.pallas_call(functools.partial(kernel, sizes), out_shape=(jax.ShapeDtyp...]
where the time goes in v3:
time: 91.1 us; the launch traced here: 91 us
  Pallas kernels  88.1 us (97%)
  local copies, waits for them, and re-layouts  2.28 us (3%)
    pallas_call x1, Pallas kernels, step(): pl.pallas_call(functools.partial(kernel, sizes), out_shape=(jax.ShapeDtyp...  88.1 us
    unnamed x4, local copies, waits for them, and re-layouts  2.28 us

profile of v3, /device:TPU:1, one launch (start us, length us, event | category | flops | bytes accessed | tf_op | source)
XLA Modules:
  0.0 91.0 jit_solution(9947668951432112334)
XLA Ops:
  0.6 88.1 %shard_map.59 = (f32[3,8,32,128]{3,2,1,0:T(8,128)}, f32[6]{0:T(128)}) custom-call(f32[8,32,128]{2,1,0:T(8,128)} %src_hbm.1, f32[8,32,128]{2,1,0:T(8,128)} %tgt_hbm.1, f32[5]{0:T(128)} %kern_hbm.1, f32[9]{0:T(128)} %smo_hbm.1), custom_call_target="tpu_custom_call" | custom-call | tf_op jit(solution)/shard_map/pallas_call | solution.py:532
  88.7 0.0 copy-start
  88.7 1.8 %copy.8 = f32[3,8,32,128]{3,2,1,0:T(8,128)} copy(f32[3,8,32,128]{3,2,1,0:T(8,128)} %get-tuple-element.4) | data formatting | bytes 786432
  90.5 0.0 copy-done
  90.5 0.5 copy.9
Async XLA Ops:
  88.7 1.8 %copy-start = (f32[6]{0:T(128)S(1)}, f32[6]{0:T(128)}, u32[]{:S(2)}) copy-start(f32[6]{0:T(128)} %get-tuple-element.5) | copy-start | bytes 76

commit v4 on v3

--- a/solution.py
+++ b/solution.py
@@ -221,18 +221,29 @@
         return tiles
 
     def x_pass(p, dst, passes):
-        for j in range(TY + 2):
+        for j in range(TY + 1):
             rows = pl.ds(8 * j, 8)
             col = [f[p, i, rows, :] for i in range(2 * R + BX)]
+            if j == 0:
+                last = pl.ds(8 * (TY + 1), 8)
+                col = [jnp.where(sub < R, f[p, i, last, :], v) for i, v in enumerate(col)]
             for i in range(BX):
                 for n, q in enumerate(passes):
-                    dst[n, i, rows, :] = q(k, lambda d: col[i + R + d])
+                    v = q(k, lambda d: col[i + R + d])
+                    dst[n, i, rows, :] = v
+                    if j == 0:
+                        dst[n, i, last, :] = v
 
     def x_pass_packed(p, dst, passes):
-        for j, z in enumerate(packed_in(p)):
+        tiles = packed_in(p)
+        tiles[0] = jnp.where(sub < R, tiles.pop(), tiles[0])
+        for j, z in enumerate(tiles):
             moved = {d: roll(z, -8 * d) for d in range(-R, R + 1)}
             for n, q in enumerate(passes):
-                dst[n, pl.ds(8 * j, 8), :] = q(k, lambda d: moved[d])
+                v = q(k, lambda d: moved[d])
+                dst[n, pl.ds(8 * j, 8), :] = v
+                if j == 0:
+                    dst[n, pl.ds(8 * (TY + 1), 8), :] = v
 
     def y_at(ref, j):
         return lambda d: ref[pl.ds(8 + 8 * j + d, 8), :]

time: 91.1 us -> 91 us (level)
  no operation moved by 1% of the time
where the time goes in v4:
time: 91 us; the launch traced here: 90.8 us
  Pallas kernels  87.9 us (97%)
  local copies, waits for them, and re-layouts  2.28 us (3%)
    pallas_call x1, Pallas kernels, step(): pl.pallas_call(functools.partial(kernel, sizes), out_shape=(jax.ShapeDtyp...  87.9 us
    unnamed x4, local copies, waits for them, and re-layouts  2.28 us

profile of v4, /device:TPU:1, one launch (start us, length us, event | category | flops | bytes accessed | tf_op | source)
XLA Modules:
  0.0 90.8 jit_solution(6906702702990373132)
XLA Ops:
  0.6 87.9 %shard_map.59 = (f32[3,8,32,128]{3,2,1,0:T(8,128)}, f32[6]{0:T(128)}) custom-call(f32[8,32,128]{2,1,0:T(8,128)} %src_hbm.1, f32[8,32,128]{2,1,0:T(8,128)} %tgt_hbm.1, f32[5]{0:T(128)} %kern_hbm.1, f32[9]{0:T(128)} %smo_hbm.1), custom_call_target="tpu_custom_call" | custom-call | tf_op jit(solution)/shard_map/pallas_call | solution.py:543
  88.6 0.0 copy-start
  88.6 1.8 %copy.8 = f32[3,8,32,128]{3,2,1,0:T(8,128)} copy(f32[3,8,32,128]{3,2,1,0:T(8,128)} %get-tuple-element.4) | data formatting | bytes 786432
  90.3 0.0 copy-done
  90.3 0.5 copy.9
Async XLA Ops:
  88.6 1.8 %copy-start = (f32[6]{0:T(128)S(1)}, f32[6]{0:T(128)}, u32[]{:S(2)}) copy-start(f32[6]{0:T(128)} %get-tuple-element.5) | copy-start | bytes 76
